TPU v7x, 32 devices: a whole 2x2x4 slice. The times are simulated.
32 devices in a mesh: gx: 4 (over z), gy: 4 (over y, x), gz: 2 (over core).
Axes of the slice: x: 2, y: 2, z: 4, core: 2. Of those that a mesh axis runs over, the one named last changes fastest.
Arguments:
- right_side: float32 [4, 96, 96, 48], P(None, 'gx', 'gy', 'gz'), may hold values from -6 to 6
- iterate: float32 [4, 96, 96, 48], P(None, 'gx', 'gy', 'gz'), may hold values from -6 to 6
- coefficient: float32 [96, 96, 48], P('gx', 'gy', 'gz'), may hold values from 0.1 to 2
- ordering: int32 [4, 4, 2, 216], P('gx', 'gy', 'gz'), may hold values from 0 to 215, as said below
- leaf_inverse: float32 [4, 4, 2, 125, 125], P('gx', 'gy', 'gz'), may hold values from -2 to 3
- leaf_first: float32 [4, 4, 2, 125, 50], P('gx', 'gy', 'gz'), may hold values from -0.5 to 0.5
- leaf_second: float32 [4, 4, 2, 125, 60], P('gx', 'gy', 'gz'), may hold values from -0.5 to 0.5
- leaf_top: float32 [4, 4, 2, 125, 72], P('gx', 'gy', 'gz'), may hold values from -0.5 to 0.5
- first_inverse: float32 [4, 4, 50, 50], P('gx', 'gy', 'gz'), may hold values from -2 to 3
- first_second: float32 [4, 4, 2, 25, 60], P('gx', 'gy', 'gz'), may hold values from -1.25 to 1.25
- first_top: float32 [4, 4, 2, 25, 72], P('gx', 'gy', 'gz'), may hold values from -1.25 to 1.25
- second_inverse: float32 [4, 240, 240], P('gx', ('gy', 'gz')), may hold values from -2 to 3
- second_top: float32 [4, 4, 2, 30, 72], P('gx', 'gy', 'gz'), may hold values from -1 to 1
- top_inverse: float32 [1152, 1152], P(('gx', 'gy', 'gz')), may hold values from -2 to 3
Outputs:
- correction: float32 [4, 96, 96, 48], P(None, 'gx', 'gy', 'gz')
Inputs may be any that keep to these rules, and one draw needn't show every extreme that they name: `ordering`: each device's row names each of its 216 coarse cells once (cell x 6^2 + y * 6 + z): first the 125 cells with x, y and z all below 5, then the 25 cells with z = 5 and x, y below it, then the 30 cells with y = 5 and x below it, then the 36 cells with x = 5, each group in any order.
All inputs are finite; a program needn't handle non-finite values.
Results may differ from a plain program's by a relative error of at most 0.0003.
Values sent between devices are 32-bit elements; how exact they have to be, the bound alone decides.
A program may use at most 64 MiB of HBM per device.

v0:
```python
import jax
import jax.numpy as jnp
from jax import lax
from jax.sharding import PartitionSpec as P

precise = lax.Precision.HIGHEST


def shifted(shard, axis, by):
    peers = lax.axis_size(axis)
    pairs = [(i, i + by) for i in range(peers) if 0 <= i + by < peers]
    return lax.ppermute(shard, axis, pairs)


def with_halo(cells, sides, width):
    for axis, dim in sides:
        count = lax.axis_size(axis)
        ends = count - 1
        head = lax.slice_in_dim(cells, 0, width, axis=dim)
        tail = lax.slice_in_dim(cells, cells.shape[dim] - width, cells.shape[dim], axis=dim)
        cells = jnp.concatenate(
            [
                lax.ppermute(tail, axis, [(i, (i + 1) % count) for i in range(ends)]),
                cells,
                lax.ppermute(head, axis, [((i + 1) % count, i) for i in range(ends)]),
            ],
            axis=dim,
        )
    return cells


def product(operand, matrix):
    return jnp.dot(operand, matrix, precision=precise, preferred_element_type=jnp.float32)


def product_back(operand, matrix):
    return lax.dot_general(
        operand,
        matrix,
        (((1,), (1,)), ((), ())),
        precision=precise,
        preferred_element_type=jnp.float32,
    )


def weigh(extended, dimension):
    length = extended.shape[dimension] - 1
    previous = lax.slice_in_dim(extended, 0, length, 2, dimension)
    centre = lax.slice_in_dim(extended, 1, length + 1, 2, dimension)
    following = lax.slice_in_dim(extended, 2, length + 1, 2, dimension)
    return 0.25 * previous + 0.5 * centre + 0.25 * following


def spread(extended, dimension):
    length = extended.shape[dimension] - 1
    current = lax.slice_in_dim(extended, 0, length, 1, dimension)
    following = lax.slice_in_dim(extended, 1, length + 1, 1, dimension)
    paired = jnp.stack([current, 0.5 * (current + following)], axis=dimension + 1)
    new_shape = list(current.shape)
    new_shape[dimension] = 2 * length
    return paired.reshape(new_shape)


def lower_rims(values):
    boundary = shifted(values[:, -1:], "gx", 1)
    values = jnp.concatenate([boundary, values], axis=1)
    boundary = shifted(values[:, :, -1:], "gy", 1)
    values = jnp.concatenate([boundary, values], axis=2)
    boundary = shifted(values[:, :, :, -1:], "gz", 1)
    return jnp.concatenate([boundary, values], axis=3)


def upper_rims(values):
    boundary = shifted(values[:, :1], "gx", -1)
    values = jnp.concatenate([values, boundary], axis=1)
    boundary = shifted(values[:, :, :1], "gy", -1)
    values = jnp.concatenate([values, boundary], axis=2)
    boundary = shifted(values[:, :, :, :1], "gz", -1)
    return jnp.concatenate([values, boundary], axis=3)


def restrict(values):
    extended = lower_rims(values)
    for dimension in (1, 2, 3):
        extended = weigh(extended, dimension)
    return extended


def prolong(values):
    extended = upper_rims(values)
    for dimension in (1, 2, 3):
        extended = spread(extended, dimension)
    return extended


def residual_of(right_side, iterate, coefficient):
    padded = with_halo(iterate, (("gx", 1), ("gy", 2), ("gz", 3)), 1)
    beside = padded[:, 2:, 1:-1, 1:-1] + padded[:, :-2, 1:-1, 1:-1]
    beside = beside + padded[:, 1:-1, 2:, 1:-1] + padded[:, 1:-1, :-2, 1:-1]
    beside = beside + padded[:, 1:-1, 1:-1, 2:] + padded[:, 1:-1, 1:-1, :-2]
    return right_side - ((6.0 + coefficient) * iterate - beside)


def per_device(
    right_side,
    iterate,
    coefficient,
    ordering,
    leaf_inverse,
    leaf_first,
    leaf_second,
    leaf_top,
    first_inverse,
    first_second,
    first_top,
    second_inverse,
    second_top,
    top_inverse,
):
    rhs_count = right_side.shape[0]
    leaf_size = leaf_inverse.shape[-1]
    first_size = first_second.shape[3]
    second_size = second_top.shape[3]
    top_size = top_inverse.shape[0]
    first_rows = first_inverse[0, 0]
    second_rows = second_inverse[0]
    first_start = lax.axis_index("gz") * first_size
    first_full = lax.all_gather(first_rows, "gz", axis=0, tiled=True)
    first_columns = lax.dynamic_slice_in_dim(first_full, first_start, first_size, 1)
    coarse = restrict(restrict(residual_of(right_side, iterate, coefficient)))
    coarse_side = coarse.shape[1]
    flattened = coarse.reshape(rhs_count, coarse_side**3)
    order_row = ordering.reshape(-1)
    chosen = jnp.take(flattened, order_row, axis=1)
    first_end = leaf_size + first_size
    second_end = first_end + second_size
    leaf_rhs = chosen[:, :leaf_size]
    first_rhs = chosen[:, leaf_size:first_end]
    second_rhs = chosen[:, first_end:second_end]
    top_rhs = chosen[:, second_end:]
    leaf_block = leaf_inverse[0, 0, 0]
    to_first = leaf_first[0, 0, 0]
    to_second = leaf_second[0, 0, 0]
    to_top = leaf_top[0, 0, 0]
    first_to_second = first_second[0, 0, 0]
    first_to_top = first_top[0, 0, 0]
    second_to_top = second_top[0, 0, 0]
    leaf_solved = product(leaf_rhs, leaf_block)
    toward = product(leaf_solved, to_first)
    arrived = shifted(toward[:, first_size:], "gz", -1)
    first_target = first_rhs - toward[:, :first_size] - arrived
    target_whole = lax.all_gather(first_target, "gz", axis=1, tiled=True)
    first_own = product(target_whole, first_columns)
    toward = product(leaf_solved, to_second) + product(first_own, first_to_second)
    arrived = shifted(toward[:, second_size:], "gy", -1)
    second_target = second_rhs - toward[:, :second_size] - arrived
    second_own = lax.psum_scatter(
        product(second_target, second_rows), ("gy", "gz"), scatter_dimension=1, tiled=True
    )
    toward = (
        product(leaf_solved, to_top)
        + product(first_own, first_to_top)
        + product(second_own, second_to_top)
    )
    arrived = shifted(toward[:, top_size:], "gx", -1)
    top_target = top_rhs - toward[:, :top_size] - arrived
    top_own = lax.psum_scatter(
        product(top_target, top_inverse), ("gx", "gy", "gz"), scatter_dimension=1, tiled=True
    )
    top_whole = lax.all_gather(top_own, ("gx", "gy", "gz"), axis=1, tiled=True)
    top_back = product_back(top_whole, top_inverse)
    top_lower = shifted(top_back, "gx", 1)
    top_pair = jnp.concatenate([top_back, top_lower], axis=1)
    second_gap = second_own - product_back(top_pair, second_to_top)
    second_whole = lax.all_gather(second_gap, ("gy", "gz"), axis=1, tiled=True)
    second_back = product_back(second_whole, second_rows)
    second_lower = shifted(second_back, "gy", 1)
    second_pair = jnp.concatenate([second_back, second_lower], axis=1)
    first_gap = (
        first_own
        - product_back(second_pair, first_to_second)
        - product_back(top_pair, first_to_top)
    )
    first_whole = lax.all_gather(first_gap, "gz", axis=1, tiled=True)
    first_back = product_back(first_whole, first_rows)
    first_lower = shifted(first_back, "gz", 1)
    first_pair = jnp.concatenate([first_back, first_lower], axis=1)
    leaf_gap = (
        leaf_solved - product_back(first_pair, to_first) - product_back(second_pair, to_second)
    )
    leaf_gap = leaf_gap - product_back(top_pair, to_top)
    leaf_back = product_back(leaf_gap, leaf_block)
    ordered = jnp.concatenate([leaf_back, first_back, second_back, top_back], axis=1)
    coarse_cells = jnp.zeros_like(ordered).at[:, order_row].set(ordered)
    coarse_grid = coarse_cells.reshape(rhs_count, coarse_side, coarse_side, coarse_side)
    return prolong(prolong(coarse_grid))


def solution(mesh):
    return jax.shard_map(
        per_device,
        mesh=mesh,
        in_specs=(
            P(None, "gx", "gy", "gz"),
            P(None, "gx", "gy", "gz"),
            P("gx", "gy", "gz"),
            P("gx", "gy", "gz", None),
            P("gx", "gy", "gz", None, None),
            P("gx", "gy", "gz", None, None),
            P("gx", "gy", "gz", None, None),
            P("gx", "gy", "gz", None, None),
            P("gx", "gy", "gz", None),
            P("gx", "gy", "gz", None, None),
            P("gx", "gy", "gz", None, None),
            P("gx", ("gy", "gz"), None),
            P("gx", "gy", "gz", None, None),
            P(("gx", "gy", "gz"), None),
        ),
        out_specs=P(None, "gx", "gy", "gz"),
        check_vma=False,
    )
```

profile of v0, /device:TPU:11, one launch (start us, length us, event | category | flops | bytes accessed | tf_op | source)
XLA Modules:
  0.0 293.7 jit_solution(13946960478446539935)
XLA Ops:
  2.9 3.2 %collective-permute-start.1 = (f32[4,1,24,24]{3,2,1,0:T(8,128)S(1)}, f32[4,1,24,24]{3,2,1,0:T(8,128)S(1)}, u32[]{:S(2)}, u32[]{:S(2)}) collective-permute-start(f32[4,1,24,24]{3,2,1,0:T(8,128)S(1)} %get-tuple-element.9), channel_id=1, source_target_pairs={{0,8},{8,16},{16,24},{1,9},{9,17},{17,25},{2,10},{10,18},{18,26},{... | collective-permute-start | bytes 27656 | tf_op jit(solution)/shard_map/ppermute | solution.py:23
  13.4 4.2 %collective-permute-start.3 = (f32[4,26,1,24]{1,3,2,0:T(8,128)S(1)}, f32[4,26,1,24]{1,3,2,0:T(8,128)S(1)}, u32[]{:S(2)}, u32[]{:S(2)}) collective-permute-start(f32[4,26,1,24]{1,3,2,0:T(8,128)S(1)} %get-tuple-element.7), channel_id=1, source_target_pairs={{0,2},{2,4},{4,6},{1,3},{3,5},{5,7},{8,10},{10,12},{12,14},{9,11},... | collective-permute-start | bytes 29960 | tf_op jit(solution)/shard_map/ppermute | solution.py:23
  19.3 4.4 %collective-permute-start.4 = (f32[4,26,26,1]{2,1,3,0:T(8,128)S(1)}, f32[4,26,26,1]{2,1,3,0:T(8,128)S(1)}, u32[]{:S(2)}, u32[]{:S(2)}) collective-permute-start(f32[4,26,26,1]{2,1,3,0:T(8,128)S(1)} %copy.147), channel_id=1, source_target_pairs={{1,0},{3,2},{5,4},{7,6},{9,8},{11,10},{13,12},{15,14},{17,16},{19,... | collective-permute-start | bytes 32456 | tf_op jit(solution)/shard_map/ppermute | solution.py:25
  28.3 9.4 %fusion.2 = f32[4,24,24,24]{1,3,2,0:T(8,128)S(1)} fusion(f32[4,24,24,24]{1,3,2,0:T(8,128)} %copy.151, f32[4,26,26,1]{1,3,2,0:T(1,128)S(1)} %copy.150, f32[4,26,1,24]{1,3,2,0:T(8,128)S(1)} %collective-permute-done.2, f32[4,26,1,24]{1,3,2,0:T(8,128)S(1)} %collective-permute-done.3, f32[4,1,24,24]{1,3,2,0:T(8,128)} %copy-done.1, ...), kind=kLoop, calls=%fused_computation.7 | loop fusion | flops 1437696 | bytes 778880 | tf_op jit(solution)/shard_map/sub | solution.py:101
  38.6 3.2 %collective-permute-start.6 = (f32[4,1,24,24]{3,2,1,0:T(8,128)S(1)}, f32[4,1,24,24]{3,2,1,0:T(8,128)S(1)}, u32[]{:S(2)}, u32[]{:S(2)}) collective-permute-start(f32[4,1,24,24]{3,2,1,0:T(8,128)S(1)} %copy.152), channel_id=1, source_target_pairs={{0,8},{8,16},{16,24},{1,9},{9,17},{17,25},{2,10},{10,18},{18,26},{... | collective-permute-start | bytes 27656 | tf_op jit(solution)/shard_map/ppermute | solution.py:12
  44.2 4.9 %collective-permute-start.7 = (f32[4,25,1,24]{1,3,2,0:T(8,128)S(1)}, f32[4,25,1,24]{1,3,2,0:T(8,128)S(1)}, u32[]{:S(2)}, u32[]{:S(2)}) collective-permute-start(f32[4,25,1,24]{1,3,2,0:T(8,128)S(1)} %pad_maximum_fusion.35), channel_id=1, source_target_pairs={{0,2},{2,4},{4,6},{1,3},{3,5},{5,7},{8,10},{10,12},{12,14},{9,11},... | collective-permute-start | bytes 28808 | tf_op jit(solution)/shard_map/ppermute | solution.py:12
  51.8 3.8 %collective-permute-done.8 = f32[4,25,25,1]{2,1,3,0:T(8,128)S(1)} collective-permute-done((f32[4,25,25,1]{2,1,3,0:T(8,128)S(1)}, f32[4,25,25,1]{2,1,3,0:T(8,128)S(1)}, u32[]{:S(2)}, u32[]{:S(2)}) %collective-permute-start.8) | collective-permute-done | bytes 10032 | tf_op jit(solution)/shard_map/ppermute | solution.py:12
  57.6 8.4 %slice.213 = f32[4,12,25,25]{1,3,2,0:T(8,128)} slice(f32[4,25,25,25]{1,3,2,0:T(8,128)S(1)} %maximum_maximum_fusion), slice={[0:4:1], [0:24:2], [0:25:1], [0:25:1]} | slice | bytes 240000 | tf_op jit(solution)/shard_map/slice | solution.py:48
  66.0 8.5 %slice.214 = f32[4,12,25,25]{1,3,2,0:T(8,128)} slice(f32[4,25,25,25]{1,3,2,0:T(8,128)S(1)} %maximum_maximum_fusion), slice={[0:4:1], [1:25:2], [0:25:1], [0:25:1]} | slice | bytes 240000 | tf_op jit(solution)/shard_map/slice | solution.py:49
  74.5 8.5 %slice.215 = f32[4,12,25,25]{1,3,2,0:T(8,128)} slice(f32[4,25,25,25]{1,3,2,0:T(8,128)S(1)} %maximum_maximum_fusion), slice={[0:4:1], [2:25:2], [0:25:1], [0:25:1]} | slice | bytes 240000 | tf_op jit(solution)/shard_map/slice | solution.py:50
  87.2 3.2 %collective-permute-start.9 = (f32[4,1,12,12]{1,3,2,0:T(8,128)S(1)}, f32[4,1,12,12]{1,3,2,0:T(8,128)S(1)}, u32[]{:S(2)}, u32[]{:S(2)}) collective-permute-start(f32[4,1,12,12]{1,3,2,0:T(8,128)S(1)} %slice.265), channel_id=1, source_target_pairs={{0,8},{8,16},{16,24},{1,9},{9,17},{17,25},{2,10},{10,18},{18,26},{... | collective-permute-start | bytes 6920 | tf_op jit(solution)/shard_map/ppermute | solution.py:12
  92.3 7.3 %collective-permute-done.9 = f32[4,1,12,12]{1,3,2,0:T(8,128)S(1)} collective-permute-done((f32[4,1,12,12]{1,3,2,0:T(8,128)S(1)}, f32[4,1,12,12]{1,3,2,0:T(8,128)S(1)}, u32[]{:S(2)}, u32[]{:S(2)}) %collective-permute-start.9) | collective-permute-done | bytes 2336 | tf_op jit(solution)/shard_map/ppermute | solution.py:12
  99.7 4.9 %collective-permute-start.10 = (f32[4,13,1,12]{1,3,2,0:T(8,128)S(1)}, f32[4,13,1,12]{1,3,2,0:T(8,128)S(1)}, u32[]{:S(2)}, u32[]{:S(2)}) collective-permute-start(f32[4,13,1,12]{1,3,2,0:T(8,128)S(1)} %pad_maximum_fusion.39), channel_id=1, source_target_pairs={{0,2},{2,4},{4,6},{1,3},{3,5},{5,7},{8,10},{10,12},{12,14},{9,11},... | collective-permute-start | bytes 7496 | tf_op jit(solution)/shard_map/ppermute | solution.py:12
  122.9 3.7 %collective-permute-done.13 = f32[4,30]{1,0:T(4,128)S(1)} collective-permute-done((f32[4,30]{1,0:T(4,128)S(1)}, f32[4,30]{1,0:T(4,128)S(1)}, u32[]{:S(2)}, u32[]{:S(2)}) %collective-permute-start.13) | collective-permute-done | bytes 512 | tf_op jit(solution)/shard_map/ppermute | solution.py:12
  126.8 11.4 %all-reduce = f32[4,240]{1,0:T(4,128)S(1)} all-reduce(f32[4,240]{1,0:T(4,128)S(1)} %fusion.36), channel_id=3, replica_groups=mesh['gx'=4,'gy'=4,'gz'=2] {'gy','gz'}, use_global_device_ids=true, to_apply=%region_0.1.clone | all-reduce | flops 960 | bytes 7680
  143.1 40.6 %all-reduce.1 = f32[4,1152]{1,0:T(4,128)S(1)} all-reduce(f32[4,1152]{1,0:T(4,128)S(1)} %fusion.68), channel_id=4, replica_groups=mesh['gx'=4,'gy'=4,'gz'=2] {'gx','gy','gz'}, use_global_device_ids=true, to_apply=%region_1.2.clone | all-reduce | flops 4608 | bytes 36864
  183.8 32.4 %all-gather.2 = f32[32,36,4]{1,2,0:T(4,128)S(1)} all-gather(f32[1,36,4]{1,2,0:T(4,128)S(1)} %dynamic-slice_bitcast_fusion), channel_id=1, replica_groups=mesh['gx'=4,'gy'=4,'gz'=2] {'gx','gy','gz'}, dimensions={0}, use_global_device_ids=true | all-gather | bytes 19008 | tf_op jit(solution)/shard_map/all_gather | solution.py:170
  218.5 6.9 %collective-permute-done.15 = f32[4,36]{1,0:T(4,128)S(1)} collective-permute-done((f32[4,36]{1,0:T(4,128)S(1)}, f32[4,36]{1,0:T(4,128)S(1)}, u32[]{:S(2)}, u32[]{:S(2)}) %collective-permute-start.15) | collective-permute-done | bytes 608 | tf_op jit(solution)/shard_map/ppermute | solution.py:12
  225.6 13.6 %all-gather.3 = f32[8,30,4]{1,2,0:T(4,128)S(1)} all-gather(f32[1,30,4]{1,2,0:T(4,128)S(1)} %fusion.9), channel_id=1, replica_groups=mesh['gx'=4,'gy'=4,'gz'=2] {'gy','gz'}, dimensions={0}, use_global_device_ids=true | all-gather | bytes 4320 | tf_op jit(solution)/shard_map/all_gather | solution.py:175
  239.4 3.1 %collective-permute-start.16 = (f32[4,30]{1,0:T(4,128)S(1)}, f32[4,30]{1,0:T(4,128)S(1)}, u32[]{:S(2)}, u32[]{:S(2)}) collective-permute-start(f32[4,30]{1,0:T(4,128)S(1)} %fusion.34), channel_id=1, source_target_pairs={{0,2},{2,4},{4,6},{1,3},{3,5},{5,7},{8,10},{10,12},{12,14},{9,11},... | collective-permute-start | bytes 1448 | tf_op jit(solution)/shard_map/ppermute | solution.py:12
  258.8 3.4 %collective-permute-done.19 = f32[4,7,1,6]{3,2,1,0:T(1,128)S(1)} collective-permute-done((f32[4,7,1,6]{3,2,1,0:T(1,128)S(1)}, f32[4,7,1,6]{3,2,1,0:T(1,128)S(1)}, u32[]{:S(2)}, u32[]{:S(2)}) %collective-permute-start.19) | collective-permute-done | bytes 704 | tf_op jit(solution)/shard_map/ppermute | solution.py:12
  262.3 4.4 %collective-permute-start.20 = (f32[4,7,7,1]{3,2,1,0:T(8,128)S(1)}, f32[4,7,7,1]{3,2,1,0:T(8,128)S(1)}, u32[]{:S(2)}, u32[]{:S(2)}) collective-permute-start(f32[4,7,7,1]{3,2,1,0:T(8,128)S(1)} %pad_maximum_fusion.26), channel_id=1, source_target_pairs={{1,0},{3,2},{5,4},{7,6},{9,8},{11,10},{13,12},{15,14},{17,16},{19,... | collective-permute-start | bytes 2360 | tf_op jit(solution)/shard_map/ppermute | solution.py:12
  275.6 8.4 %collective-permute-done.22 = f32[4,13,1,12]{2,0,3,1:T(4,128)S(1)} collective-permute-done((f32[4,13,1,12]{2,0,3,1:T(4,128)S(1)}, f32[4,13,1,12]{2,0,3,1:T(4,128)S(1)}, u32[]{:S(2)}, u32[]{:S(2)}) %collective-permute-start.22) | collective-permute-done | bytes 2528 | tf_op jit(solution)/shard_map/ppermute | solution.py:12
  284.1 4.3 %collective-permute-start.23 = (f32[4,13,13,1]{2,0,3,1:T(4,128)S(1)}, f32[4,13,13,1]{2,0,3,1:T(4,128)S(1)}, u32[]{:S(2)}, u32[]{:S(2)}) collective-permute-start(f32[4,13,13,1]{2,0,3,1:T(4,128)S(1)} %pad_maximum_fusion.40), channel_id=1, source_target_pairs={{1,0},{3,2},{5,4},{7,6},{9,8},{11,10},{13,12},{15,14},{17,16},{19,... | collective-permute-start | bytes 8120 | tf_op jit(solution)/shard_map/ppermute | solution.py:12
  (186 shorter events, 86.1 us)
Async XLA Ops:
  0.9 6.9 %collective-permute-start = (f32[4,1,24,24]{3,2,1,0:T(8,128)S(1)}, f32[4,1,24,24]{3,2,1,0:T(8,128)S(1)}, u32[]{:S(2)}, u32[]{:S(2)}) collective-permute-start(f32[4,1,24,24]{3,2,1,0:T(8,128)S(1)} %get-tuple-element.10), channel_id=1, source_target_pairs={{8,0},{16,8},{24,16},{9,1},{17,9},{25,17},{10,2},{18,10},{26,18},{... | collective-permute-start | bytes 27656 | tf_op jit(solution)/shard_map/ppermute | solution.py:25
  2.9 5.5 %collective-permute-start.1 = (f32[4,1,24,24]{3,2,1,0:T(8,128)S(1)}, f32[4,1,24,24]{3,2,1,0:T(8,128)S(1)}, u32[]{:S(2)}, u32[]{:S(2)}) collective-permute-start(f32[4,1,24,24]{3,2,1,0:T(8,128)S(1)} %get-tuple-element.9), channel_id=1, source_target_pairs={{0,8},{8,16},{16,24},{1,9},{9,17},{17,25},{2,10},{10,18},{18,26},{... | collective-permute-start | bytes 27656 | tf_op jit(solution)/shard_map/ppermute | solution.py:23
  11.2 6.3 %collective-permute-start.2 = (f32[4,26,1,24]{1,3,2,0:T(8,128)S(1)}, f32[4,26,1,24]{1,3,2,0:T(8,128)S(1)}, u32[]{:S(2)}, u32[]{:S(2)}) collective-permute-start(f32[4,26,1,24]{1,3,2,0:T(8,128)S(1)} %get-tuple-element.8), channel_id=1, source_target_pairs={{2,0},{4,2},{6,4},{3,1},{5,3},{7,5},{10,8},{12,10},{14,12},{11,9},... | collective-permute-start | bytes 29960 | tf_op jit(solution)/shard_map/ppermute | solution.py:25
  13.4 5.3 %collective-permute-start.3 = (f32[4,26,1,24]{1,3,2,0:T(8,128)S(1)}, f32[4,26,1,24]{1,3,2,0:T(8,128)S(1)}, u32[]{:S(2)}, u32[]{:S(2)}) collective-permute-start(f32[4,26,1,24]{1,3,2,0:T(8,128)S(1)} %get-tuple-element.7), channel_id=1, source_target_pairs={{0,2},{2,4},{4,6},{1,3},{3,5},{5,7},{8,10},{10,12},{12,14},{9,11},... | collective-permute-start | bytes 29960 | tf_op jit(solution)/shard_map/ppermute | solution.py:23
  19.3 8.7 %collective-permute-start.4 = (f32[4,26,26,1]{2,1,3,0:T(8,128)S(1)}, f32[4,26,26,1]{2,1,3,0:T(8,128)S(1)}, u32[]{:S(2)}, u32[]{:S(2)}) collective-permute-start(f32[4,26,26,1]{2,1,3,0:T(8,128)S(1)} %copy.147), channel_id=1, source_target_pairs={{1,0},{3,2},{5,4},{7,6},{9,8},{11,10},{13,12},{15,14},{17,16},{19,... | collective-permute-start | bytes 32456 | tf_op jit(solution)/shard_map/ppermute | solution.py:25
  23.9 4.3 %collective-permute-start.5 = (f32[4,26,26,1]{2,1,3,0:T(8,128)S(1)}, f32[4,26,26,1]{2,1,3,0:T(8,128)S(1)}, u32[]{:S(2)}, u32[]{:S(2)}) collective-permute-start(f32[4,26,26,1]{2,1,3,0:T(8,128)S(1)} %copy.149), channel_id=1, source_target_pairs={{0,1},{2,3},{4,5},{6,7},{8,9},{10,11},{12,13},{14,15},{16,17},{18,... | collective-permute-start | bytes 32456 | tf_op jit(solution)/shard_map/ppermute | solution.py:23
  38.6 4.8 %collective-permute-start.6 = (f32[4,1,24,24]{3,2,1,0:T(8,128)S(1)}, f32[4,1,24,24]{3,2,1,0:T(8,128)S(1)}, u32[]{:S(2)}, u32[]{:S(2)}) collective-permute-start(f32[4,1,24,24]{3,2,1,0:T(8,128)S(1)} %copy.152), channel_id=1, source_target_pairs={{0,8},{8,16},{16,24},{1,9},{9,17},{17,25},{2,10},{10,18},{18,26},{... | collective-permute-start | bytes 27656 | tf_op jit(solution)/shard_map/ppermute | solution.py:12
  44.2 6.0 %collective-permute-start.7 = (f32[4,25,1,24]{1,3,2,0:T(8,128)S(1)}, f32[4,25,1,24]{1,3,2,0:T(8,128)S(1)}, u32[]{:S(2)}, u32[]{:S(2)}) collective-permute-start(f32[4,25,1,24]{1,3,2,0:T(8,128)S(1)} %pad_maximum_fusion.35), channel_id=1, source_target_pairs={{0,2},{2,4},{4,6},{1,3},{3,5},{5,7},{8,10},{10,12},{12,14},{9,11},... | collective-permute-start | bytes 28808 | tf_op jit(solution)/shard_map/ppermute | solution.py:12
  50.5 5.1 %collective-permute-start.8 = (f32[4,25,25,1]{2,1,3,0:T(8,128)S(1)}, f32[4,25,25,1]{2,1,3,0:T(8,128)S(1)}, u32[]{:S(2)}, u32[]{:S(2)}) collective-permute-start(f32[4,25,25,1]{2,1,3,0:T(8,128)S(1)} %copy.154), channel_id=1, source_target_pairs={{0,1},{2,3},{4,5},{6,7},{8,9},{10,11},{12,13},{14,15},{16,17},{18,... | collective-permute-start | bytes 30008 | tf_op jit(solution)/shard_map/ppermute | solution.py:12
  87.2 12.4 %collective-permute-start.9 = (f32[4,1,12,12]{1,3,2,0:T(8,128)S(1)}, f32[4,1,12,12]{1,3,2,0:T(8,128)S(1)}, u32[]{:S(2)}, u32[]{:S(2)}) collective-permute-start(f32[4,1,12,12]{1,3,2,0:T(8,128)S(1)} %slice.265), channel_id=1, source_target_pairs={{0,8},{8,16},{16,24},{1,9},{9,17},{17,25},{2,10},{10,18},{18,26},{... | collective-permute-start | bytes 6920 | tf_op jit(solution)/shard_map/ppermute | solution.py:12
  99.7 5.9 %collective-permute-start.10 = (f32[4,13,1,12]{1,3,2,0:T(8,128)S(1)}, f32[4,13,1,12]{1,3,2,0:T(8,128)S(1)}, u32[]{:S(2)}, u32[]{:S(2)}) collective-permute-start(f32[4,13,1,12]{1,3,2,0:T(8,128)S(1)} %pad_maximum_fusion.39), channel_id=1, source_target_pairs={{0,2},{2,4},{4,6},{1,3},{3,5},{5,7},{8,10},{10,12},{12,14},{9,11},... | collective-permute-start | bytes 7496 | tf_op jit(solution)/shard_map/ppermute | solution.py:12
  105.7 3.8 %collective-permute-start.11 = (f32[4,13,13,1]{1,3,2,0:T(1,128)S(1)}, f32[4,13,13,1]{1,3,2,0:T(1,128)S(1)}, u32[]{:S(2)}, u32[]{:S(2)}) collective-permute-start(f32[4,13,13,1]{1,3,2,0:T(1,128)S(1)} %pad_maximum_fusion.42), channel_id=1, source_target_pairs={{0,1},{2,3},{4,5},{6,7},{8,9},{10,11},{12,13},{14,15},{16,17},{18,... | collective-permute-start | bytes 8120 | tf_op jit(solution)/shard_map/ppermute | solution.py:12
  115.0 3.4 %collective-permute-start.12 = (f32[4,25]{1,0:T(4,128)S(1)}, f32[4,25]{1,0:T(4,128)S(1)}, u32[]{:S(2)}, u32[]{:S(2)}) collective-permute-start(f32[4,25]{1,0:T(4,128)S(1)} %slice.237), channel_id=1, source_target_pairs={{1,0},{3,2},{5,4},{7,6},{9,8},{11,10},{13,12},{15,14},{17,16},{19,... | collective-permute-start | bytes 1208 | tf_op jit(solution)/shard_map/ppermute | solution.py:12
  120.8 5.8 %collective-permute-start.13 = (f32[4,30]{1,0:T(4,128)S(1)}, f32[4,30]{1,0:T(4,128)S(1)}, u32[]{:S(2)}, u32[]{:S(2)}) collective-permute-start(f32[4,30]{1,0:T(4,128)S(1)} %slice.240), channel_id=1, source_target_pairs={{2,0},{4,2},{6,4},{3,1},{5,3},{7,5},{10,8},{12,10},{14,12},{11,9},... | collective-permute-start | bytes 1448 | tf_op jit(solution)/shard_map/ppermute | solution.py:12
  138.5 4.3 %collective-permute-start.14 = (f32[4,36]{1,0:T(4,128)S(1)}, f32[4,36]{1,0:T(4,128)S(1)}, u32[]{:S(2)}, u32[]{:S(2)}) collective-permute-start(f32[4,36]{1,0:T(4,128)S(1)} %slice.243), channel_id=1, source_target_pairs={{8,0},{16,8},{24,16},{9,1},{17,9},{25,17},{10,2},{18,10},{26,18},{... | collective-permute-start | bytes 1736 | tf_op jit(solution)/shard_map/ppermute | solution.py:12
  216.5 8.9 %collective-permute-start.15 = (f32[4,36]{1,0:T(4,128)S(1)}, f32[4,36]{1,0:T(4,128)S(1)}, u32[]{:S(2)}, u32[]{:S(2)}) collective-permute-start(f32[4,36]{1,0:T(4,128)S(1)} %fusion.86), channel_id=1, source_target_pairs={{0,8},{8,16},{16,24},{1,9},{9,17},{17,25},{2,10},{10,18},{18,26},{... | collective-permute-start | bytes 1736 | tf_op jit(solution)/shard_map/ppermute | solution.py:12
  239.4 4.3 %collective-permute-start.16 = (f32[4,30]{1,0:T(4,128)S(1)}, f32[4,30]{1,0:T(4,128)S(1)}, u32[]{:S(2)}, u32[]{:S(2)}) collective-permute-start(f32[4,30]{1,0:T(4,128)S(1)} %fusion.34), channel_id=1, source_target_pairs={{0,2},{2,4},{4,6},{1,3},{3,5},{5,7},{8,10},{10,12},{12,14},{9,11},... | collective-permute-start | bytes 1448 | tf_op jit(solution)/shard_map/ppermute | solution.py:12
  247.2 3.1 %collective-permute-start.17 = (f32[4,25]{1,0:T(4,128)S(1)}, f32[4,25]{1,0:T(4,128)S(1)}, u32[]{:S(2)}, u32[]{:S(2)}) collective-permute-start(f32[4,25]{1,0:T(4,128)S(1)} %fusion.50), channel_id=1, source_target_pairs={{0,1},{2,3},{4,5},{6,7},{8,9},{10,11},{12,13},{14,15},{16,17},{18,... | collective-permute-start | bytes 1208 | tf_op jit(solution)/shard_map/ppermute | solution.py:12
  252.4 4.5 %collective-permute-start.18 = (f32[4,1,6,6]{3,2,1,0:T(8,128)S(1)}, f32[4,1,6,6]{3,2,1,0:T(8,128)S(1)}, u32[]{:S(2)}, u32[]{:S(2)}) collective-permute-start(f32[4,1,6,6]{3,2,1,0:T(8,128)S(1)} %slice.270), channel_id=1, source_target_pairs={{8,0},{16,8},{24,16},{9,1},{17,9},{25,17},{10,2},{18,10},{26,18},{... | collective-permute-start | bytes 1736 | tf_op jit(solution)/shard_map/ppermute | solution.py:12
  256.9 5.4 %collective-permute-start.19 = (f32[4,7,1,6]{3,2,1,0:T(1,128)S(1)}, f32[4,7,1,6]{3,2,1,0:T(1,128)S(1)}, u32[]{:S(2)}, u32[]{:S(2)}) collective-permute-start(f32[4,7,1,6]{3,2,1,0:T(1,128)S(1)} %slice.271), channel_id=1, source_target_pairs={{2,0},{4,2},{6,4},{3,1},{5,3},{7,5},{10,8},{12,10},{14,12},{11,9},... | collective-permute-start | bytes 2024 | tf_op jit(solution)/shard_map/ppermute | solution.py:12
  262.3 5.3 %collective-permute-start.20 = (f32[4,7,7,1]{3,2,1,0:T(8,128)S(1)}, f32[4,7,7,1]{3,2,1,0:T(8,128)S(1)}, u32[]{:S(2)}, u32[]{:S(2)}) collective-permute-start(f32[4,7,7,1]{3,2,1,0:T(8,128)S(1)} %pad_maximum_fusion.26), channel_id=1, source_target_pairs={{1,0},{3,2},{5,4},{7,6},{9,8},{11,10},{13,12},{15,14},{17,16},{19,... | collective-permute-start | bytes 2360 | tf_op jit(solution)/shard_map/ppermute | solution.py:12
  269.0 4.6 %collective-permute-start.21 = (f32[4,1,12,12]{2,0,3,1:T(4,128)S(1)}, f32[4,1,12,12]{2,0,3,1:T(4,128)S(1)}, u32[]{:S(2)}, u32[]{:S(2)}) collective-permute-start(f32[4,1,12,12]{2,0,3,1:T(4,128)S(1)} %slice.278), channel_id=1, source_target_pairs={{8,0},{16,8},{24,16},{9,1},{17,9},{25,17},{10,2},{18,10},{26,18},{... | collective-permute-start | bytes 6920 | tf_op jit(solution)/shard_map/ppermute | solution.py:12
  273.7 10.4 %collective-permute-start.22 = (f32[4,13,1,12]{2,0,3,1:T(4,128)S(1)}, f32[4,13,1,12]{2,0,3,1:T(4,128)S(1)}, u32[]{:S(2)}, u32[]{:S(2)}) collective-permute-start(f32[4,13,1,12]{2,0,3,1:T(4,128)S(1)} %pad_maximum_fusion.22), channel_id=1, source_target_pairs={{2,0},{4,2},{6,4},{3,1},{5,3},{7,5},{10,8},{12,10},{14,12},{11,9},... | collective-permute-start | bytes 7496 | tf_op jit(solution)/shard_map/ppermute | solution.py:12
  284.1 5.1 %collective-permute-start.23 = (f32[4,13,13,1]{2,0,3,1:T(4,128)S(1)}, f32[4,13,13,1]{2,0,3,1:T(4,128)S(1)}, u32[]{:S(2)}, u32[]{:S(2)}) collective-permute-start(f32[4,13,13,1]{2,0,3,1:T(4,128)S(1)} %pad_maximum_fusion.40), channel_id=1, source_target_pairs={{1,0},{3,2},{5,4},{7,6},{9,8},{11,10},{13,12},{15,14},{17,16},{19,... | collective-permute-start | bytes 8120 | tf_op jit(solution)/shard_map/ppermute | solution.py:12
  (16 other events, 285.5 us)
where the time goes:
time: 295 us; the launch traced here: 294 us
  blocking collectives  105 us (36%)
  starting transfers between devices  65.4 us (22%)
  waiting for transfers between devices  52 us (18%)
  local copies, waits for them, and re-layouts  48.2 us (16%)
  other arithmetic  18.5 us (6%)
  matrix products  3.58 us (1%)
    unnamed x2, blocking collectives  52.1 us
    ppermute x18, waiting for transfers between devices, shifted(): return lax.ppermute(shard, axis, pairs)  50.9 us
    ppermute x18, starting transfers between devices, shifted(): return lax.ppermute(shard, axis, pairs)  48 us
    all_gather x1, blocking collectives, per_device(): top_whole = lax.all_gather(top_own, ('gx', 'gy', 'gz'), axis=1, tiled=True)  32.4 us
    all_gather x1, blocking collectives, per_device(): second_whole = lax.all_gather(second_gap, ('gy', 'gz'), axis=1, tiled=True)  13.6 us
    slice x4, local copies, waits for them, and re-layouts, weigh(): following = lax.slice_in_dim(extended, 2, length + 1, 2, dimension)  9.86 us
    slice x4, local copies, waits for them, and re-layouts, weigh(): centre = lax.slice_in_dim(extended, 1, length + 1, 2, dimension)  9.85 us
    slice x4, local copies, waits for them, and re-layouts, weigh(): previous = lax.slice_in_dim(extended, 0, length, 2, dimension)  9.6 us
  transfers between devices with their start and end apart: 24, of which 19 were waited for; matrix products, arithmetic and copies ran while one was open for 2% of the time, Pallas kernels for 0%

commit v1 on v0

--- a/solution.py
+++ b/solution.py
@@ -167,7 +167,12 @@
     top_own = lax.psum_scatter(
         product(top_target, top_inverse), ("gx", "gy", "gz"), scatter_dimension=1, tiled=True
     )
-    top_whole = lax.all_gather(top_own, ("gx", "gy", "gz"), axis=1, tiled=True)
+    top_whole = jnp.concatenate(
+        lax.all_to_all(
+            jnp.stack([top_own] * lax.axis_size(("gx", "gy", "gz"))), ("gx", "gy", "gz"), 0, 0
+        ),
+        axis=1,
+    )
     top_back = product_back(top_whole, top_inverse)
     top_lower = shifted(top_back, "gx", 1)
     top_pair = jnp.concatenate([top_back, top_lower], axis=1)

time: 295 us -> 268 us (0.908)
  blocking collectives: 105 us -> 81.2 us
  waiting for transfers between devices: 52 us -> 47.2 us
    all_gather x1 -> x0, blocking collectives: 32.4 us -> none  [per_device(): top_whole = lax.all_gather(top_own, ('gx', 'gy', 'gz'), axis=1, tiled=True)]
    all_to_all x0 -> x1, blocking collectives: none -> 12.3 us  [per_device(): lax.all_to_all(jnp.stack([top_own] * lax.axis_size(('gx', 'gy', 'gz'))),...]
    ppermute x18, waiting for transfers between devices: 50.9 us -> 46.1 us  [shifted(): return lax.ppermute(shard, axis, pairs)]
    all_gather x1, blocking collectives: 13.6 us -> 10.3 us  [per_device(): second_whole = lax.all_gather(second_gap, ('gy', 'gz'), axis=1, tiled=True)]
  transfers between devices with their start and end apart: 24 -> 24, of which waited for: 19 -> 19; matrix products, arithmetic and copies ran while one was open for 2% -> 3% of each run, Pallas kernels for 0% -> 0%
where the time goes in v1:
time: 268 us; the launch traced here: 267 us
  blocking collectives  81.2 us (30%)
  starting transfers between devices  65.7 us (25%)
  local copies, waits for them, and re-layouts  49 us (18%)
  waiting for transfers between devices  47.2 us (18%)
  other arithmetic  19.2 us (7%)
  matrix products  3.58 us (1%)
    unnamed x2, blocking collectives  52.1 us
    ppermute x18, starting transfers between devices, shifted(): return lax.ppermute(shard, axis, pairs)  48.4 us
    ppermute x18, waiting for transfers between devices, shifted(): return lax.ppermute(shard, axis, pairs)  46.1 us
    all_to_all x1, blocking collectives, per_device(): lax.all_to_all(jnp.stack([top_own] * lax.axis_size(('gx', 'gy', 'gz'))),...  12.3 us
    all_gather x1, blocking collectives, per_device(): second_whole = lax.all_gather(second_gap, ('gy', 'gz'), axis=1, tiled=True)  10.3 us
    slice x4, local copies, waits for them, and re-layouts, weigh(): following = lax.slice_in_dim(extended, 2, length + 1, 2, dimension)  9.85 us
    slice x4, local copies, waits for them, and re-layouts, weigh(): centre = lax.slice_in_dim(extended, 1, length + 1, 2, dimension)  9.85 us
    slice x4, local copies, waits for them, and re-layouts, weigh(): previous = lax.slice_in_dim(extended, 0, length, 2, dimension)  9.58 us
  transfers between devices with their start and end apart: 24, of which 19 were waited for; matrix products, arithmetic and copies ran while one was open for 3% of the time, Pallas kernels for 0%

profile of v1, /device:TPU:11, one launch (start us, length us, event | category | flops | bytes accessed | tf_op | source)
XLA Modules:
  0.0 267.4 jit_solution(4160146149028336174)
XLA Ops:
  2.9 3.2 %collective-permute-start.1 = (f32[4,1,24,24]{3,2,1,0:T(8,128)S(1)}, f32[4,1,24,24]{3,2,1,0:T(8,128)S(1)}, u32[]{:S(2)}, u32[]{:S(2)}) collective-permute-start(f32[4,1,24,24]{3,2,1,0:T(8,128)S(1)} %get-tuple-element.9), channel_id=1, source_target_pairs={{0,8},{8,16},{16,24},{1,9},{9,17},{17,25},{2,10},{10,18},{18,26},{... | collective-permute-start | bytes 27656 | tf_op jit(solution)/shard_map/ppermute | solution.py:23
  13.4 4.2 %collective-permute-start.3 = (f32[4,26,1,24]{1,3,2,0:T(8,128)S(1)}, f32[4,26,1,24]{1,3,2,0:T(8,128)S(1)}, u32[]{:S(2)}, u32[]{:S(2)}) collective-permute-start(f32[4,26,1,24]{1,3,2,0:T(8,128)S(1)} %get-tuple-element.7), channel_id=1, source_target_pairs={{0,2},{2,4},{4,6},{1,3},{3,5},{5,7},{8,10},{10,12},{12,14},{9,11},... | collective-permute-start | bytes 29960 | tf_op jit(solution)/shard_map/ppermute | solution.py:23
  19.3 4.4 %collective-permute-start.4 = (f32[4,26,26,1]{2,1,3,0:T(8,128)S(1)}, f32[4,26,26,1]{2,1,3,0:T(8,128)S(1)}, u32[]{:S(2)}, u32[]{:S(2)}) collective-permute-start(f32[4,26,26,1]{2,1,3,0:T(8,128)S(1)} %copy.145), channel_id=1, source_target_pairs={{1,0},{3,2},{5,4},{7,6},{9,8},{11,10},{13,12},{15,14},{17,16},{19,... | collective-permute-start | bytes 32456 | tf_op jit(solution)/shard_map/ppermute | solution.py:25
  28.3 9.4 %fusion.2 = f32[4,24,24,24]{1,3,2,0:T(8,128)S(1)} fusion(f32[4,24,24,24]{1,3,2,0:T(8,128)} %copy.149, f32[4,26,26,1]{1,3,2,0:T(1,128)S(1)} %copy.148, f32[4,26,1,24]{1,3,2,0:T(8,128)S(1)} %collective-permute-done.2, f32[4,26,1,24]{1,3,2,0:T(8,128)S(1)} %collective-permute-done.3, f32[4,1,24,24]{1,3,2,0:T(8,128)} %copy-done.1, ...), kind=kLoop, calls=%fused_computation.7 | loop fusion | flops 1437696 | bytes 778880 | tf_op jit(solution)/shard_map/sub | solution.py:101
  38.6 3.2 %collective-permute-start.6 = (f32[4,1,24,24]{3,2,1,0:T(8,128)S(1)}, f32[4,1,24,24]{3,2,1,0:T(8,128)S(1)}, u32[]{:S(2)}, u32[]{:S(2)}) collective-permute-start(f32[4,1,24,24]{3,2,1,0:T(8,128)S(1)} %copy.150), channel_id=1, source_target_pairs={{0,8},{8,16},{16,24},{1,9},{9,17},{17,25},{2,10},{10,18},{18,26},{... | collective-permute-start | bytes 27656 | tf_op jit(solution)/shard_map/ppermute | solution.py:12
  44.2 4.9 %collective-permute-start.7 = (f32[4,25,1,24]{1,3,2,0:T(8,128)S(1)}, f32[4,25,1,24]{1,3,2,0:T(8,128)S(1)}, u32[]{:S(2)}, u32[]{:S(2)}) collective-permute-start(f32[4,25,1,24]{1,3,2,0:T(8,128)S(1)} %pad_maximum_fusion.35), channel_id=1, source_target_pairs={{0,2},{2,4},{4,6},{1,3},{3,5},{5,7},{8,10},{10,12},{12,14},{9,11},... | collective-permute-start | bytes 28808 | tf_op jit(solution)/shard_map/ppermute | solution.py:12
  51.8 3.8 %collective-permute-done.8 = f32[4,25,25,1]{2,1,3,0:T(8,128)S(1)} collective-permute-done((f32[4,25,25,1]{2,1,3,0:T(8,128)S(1)}, f32[4,25,25,1]{2,1,3,0:T(8,128)S(1)}, u32[]{:S(2)}, u32[]{:S(2)}) %collective-permute-start.8) | collective-permute-done | bytes 10032 | tf_op jit(solution)/shard_map/ppermute | solution.py:12
  57.6 8.4 %slice.213 = f32[4,12,25,25]{1,3,2,0:T(8,128)} slice(f32[4,25,25,25]{1,3,2,0:T(8,128)S(1)} %maximum_maximum_fusion), slice={[0:4:1], [0:24:2], [0:25:1], [0:25:1]} | slice | bytes 240000 | tf_op jit(solution)/shard_map/slice | solution.py:48
  66.0 8.5 %slice.214 = f32[4,12,25,25]{1,3,2,0:T(8,128)} slice(f32[4,25,25,25]{1,3,2,0:T(8,128)S(1)} %maximum_maximum_fusion), slice={[0:4:1], [1:25:2], [0:25:1], [0:25:1]} | slice | bytes 240000 | tf_op jit(solution)/shard_map/slice | solution.py:49
  74.5 8.5 %slice.215 = f32[4,12,25,25]{1,3,2,0:T(8,128)} slice(f32[4,25,25,25]{1,3,2,0:T(8,128)S(1)} %maximum_maximum_fusion), slice={[0:4:1], [2:25:2], [0:25:1], [0:25:1]} | slice | bytes 240000 | tf_op jit(solution)/shard_map/slice | solution.py:50
  83.1 3.0 %multiply_add_fusion = f32[4,12,25,25]{1,3,2,0:T(8,128)S(1)} fusion(f32[4,12,25,25]{1,3,2,0:T(8,128)} %slice.215, f32[4,12,25,25]{1,3,2,0:T(8,128)} %slice.214, f32[4,12,25,25]{1,3,2,0:T(8,128)} %slice.213), kind=kLoop, calls=%fused_computation.3 | loop fusion | flops 150000 | bytes 480000 | tf_op jit(solution)/shard_map/add | solution.py:51
  87.2 3.2 %collective-permute-start.9 = (f32[4,1,12,12]{1,3,2,0:T(8,128)S(1)}, f32[4,1,12,12]{1,3,2,0:T(8,128)S(1)}, u32[]{:S(2)}, u32[]{:S(2)}) collective-permute-start(f32[4,1,12,12]{1,3,2,0:T(8,128)S(1)} %slice.265), channel_id=1, source_target_pairs={{0,8},{8,16},{16,24},{1,9},{9,17},{17,25},{2,10},{10,18},{18,26},{... | collective-permute-start | bytes 6920 | tf_op jit(solution)/shard_map/ppermute | solution.py:12
  92.3 7.3 %collective-permute-done.9 = f32[4,1,12,12]{1,3,2,0:T(8,128)S(1)} collective-permute-done((f32[4,1,12,12]{1,3,2,0:T(8,128)S(1)}, f32[4,1,12,12]{1,3,2,0:T(8,128)S(1)}, u32[]{:S(2)}, u32[]{:S(2)}) %collective-permute-start.9) | collective-permute-done | bytes 2336 | tf_op jit(solution)/shard_map/ppermute | solution.py:12
  99.7 4.9 %collective-permute-start.10 = (f32[4,13,1,12]{1,3,2,0:T(8,128)S(1)}, f32[4,13,1,12]{1,3,2,0:T(8,128)S(1)}, u32[]{:S(2)}, u32[]{:S(2)}) collective-permute-start(f32[4,13,1,12]{1,3,2,0:T(8,128)S(1)} %pad_maximum_fusion.39), channel_id=1, source_target_pairs={{0,2},{2,4},{4,6},{1,3},{3,5},{5,7},{8,10},{10,12},{12,14},{9,11},... | collective-permute-start | bytes 7496 | tf_op jit(solution)/shard_map/ppermute | solution.py:12
  122.9 3.7 %collective-permute-done.13 = f32[4,30]{1,0:T(4,128)S(1)} collective-permute-done((f32[4,30]{1,0:T(4,128)S(1)}, f32[4,30]{1,0:T(4,128)S(1)}, u32[]{:S(2)}, u32[]{:S(2)}) %collective-permute-start.13) | collective-permute-done | bytes 512 | tf_op jit(solution)/shard_map/ppermute | solution.py:12
  126.8 11.4 %all-reduce = f32[4,240]{1,0:T(4,128)S(1)} all-reduce(f32[4,240]{1,0:T(4,128)S(1)} %fusion.36), channel_id=3, replica_groups=mesh['gx'=4,'gy'=4,'gz'=2] {'gy','gz'}, use_global_device_ids=true, to_apply=%region_0.1.clone | all-reduce | flops 960 | bytes 7680
  143.1 40.6 %all-reduce.1 = f32[4,1152]{1,0:T(4,128)S(1)} all-reduce(f32[4,1152]{1,0:T(4,128)S(1)} %fusion.68), channel_id=4, replica_groups=mesh['gx'=4,'gy'=4,'gz'=2] {'gx','gy','gz'}, use_global_device_ids=true, to_apply=%region_1.2.clone | all-reduce | flops 4608 | bytes 36864
  184.0 12.3 %all_to_all.5 = f32[32,1,144]{2,1,0:T(1,128)S(1)} all-to-all(f32[32,1,144]{2,1,0:T(1,128)S(1)} %reshape.115), channel_id=1, replica_groups=mesh['gx'=4,'gy'=4,'gz'=2] {'gx','gy','gz'}, dimensions={0} | all-to-all | bytes 36864 | tf_op jit(solution)/shard_map/all_to_all | solution.py:171
  202.5 10.3 %all-gather.2 = f32[8,30,4]{1,2,0:T(4,128)S(1)} all-gather(f32[1,30,4]{1,2,0:T(4,128)S(1)} %fusion.9), channel_id=1, replica_groups=mesh['gx'=4,'gy'=4,'gz'=2] {'gy','gz'}, dimensions={0}, use_global_device_ids=true | all-gather | bytes 4320 | tf_op jit(solution)/shard_map/all_gather | solution.py:180
  213.1 3.1 %collective-permute-start.16 = (f32[4,30]{1,0:T(4,128)S(1)}, f32[4,30]{1,0:T(4,128)S(1)}, u32[]{:S(2)}, u32[]{:S(2)}) collective-permute-start(f32[4,30]{1,0:T(4,128)S(1)} %fusion.34), channel_id=1, source_target_pairs={{0,2},{2,4},{4,6},{1,3},{3,5},{5,7},{8,10},{10,12},{12,14},{9,11},... | collective-permute-start | bytes 1448 | tf_op jit(solution)/shard_map/ppermute | solution.py:12
  232.5 3.4 %collective-permute-done.19 = f32[4,7,1,6]{3,2,1,0:T(1,128)S(1)} collective-permute-done((f32[4,7,1,6]{3,2,1,0:T(1,128)S(1)}, f32[4,7,1,6]{3,2,1,0:T(1,128)S(1)}, u32[]{:S(2)}, u32[]{:S(2)}) %collective-permute-start.19) | collective-permute-done | bytes 704 | tf_op jit(solution)/shard_map/ppermute | solution.py:12
  236.0 4.4 %collective-permute-start.20 = (f32[4,7,7,1]{3,2,1,0:T(8,128)S(1)}, f32[4,7,7,1]{3,2,1,0:T(8,128)S(1)}, u32[]{:S(2)}, u32[]{:S(2)}) collective-permute-start(f32[4,7,7,1]{3,2,1,0:T(8,128)S(1)} %pad_maximum_fusion.26), channel_id=1, source_target_pairs={{1,0},{3,2},{5,4},{7,6},{9,8},{11,10},{13,12},{15,14},{17,16},{19,... | collective-permute-start | bytes 2360 | tf_op jit(solution)/shard_map/ppermute | solution.py:12
  249.3 8.4 %collective-permute-done.22 = f32[4,13,1,12]{2,0,3,1:T(4,128)S(1)} collective-permute-done((f32[4,13,1,12]{2,0,3,1:T(4,128)S(1)}, f32[4,13,1,12]{2,0,3,1:T(4,128)S(1)}, u32[]{:S(2)}, u32[]{:S(2)}) %collective-permute-start.22) | collective-permute-done | bytes 2528 | tf_op jit(solution)/shard_map/ppermute | solution.py:12
  257.8 4.3 %collective-permute-start.23 = (f32[4,13,13,1]{2,0,3,1:T(4,128)S(1)}, f32[4,13,13,1]{2,0,3,1:T(4,128)S(1)}, u32[]{:S(2)}, u32[]{:S(2)}) collective-permute-start(f32[4,13,13,1]{2,0,3,1:T(4,128)S(1)} %pad_maximum_fusion.40), channel_id=1, source_target_pairs={{1,0},{3,2},{5,4},{7,6},{9,8},{11,10},{13,12},{15,14},{17,16},{19,... | collective-permute-start | bytes 8120 | tf_op jit(solution)/shard_map/ppermute | solution.py:12
  (191 shorter events, 87.0 us)
Async XLA Ops:
  0.9 6.9 %collective-permute-start = (f32[4,1,24,24]{3,2,1,0:T(8,128)S(1)}, f32[4,1,24,24]{3,2,1,0:T(8,128)S(1)}, u32[]{:S(2)}, u32[]{:S(2)}) collective-permute-start(f32[4,1,24,24]{3,2,1,0:T(8,128)S(1)} %get-tuple-element.10), channel_id=1, source_target_pairs={{8,0},{16,8},{24,16},{9,1},{17,9},{25,17},{10,2},{18,10},{26,18},{... | collective-permute-start | bytes 27656 | tf_op jit(solution)/shard_map/ppermute | solution.py:25
  2.9 5.5 %collective-permute-start.1 = (f32[4,1,24,24]{3,2,1,0:T(8,128)S(1)}, f32[4,1,24,24]{3,2,1,0:T(8,128)S(1)}, u32[]{:S(2)}, u32[]{:S(2)}) collective-permute-start(f32[4,1,24,24]{3,2,1,0:T(8,128)S(1)} %get-tuple-element.9), channel_id=1, source_target_pairs={{0,8},{8,16},{16,24},{1,9},{9,17},{17,25},{2,10},{10,18},{18,26},{... | collective-permute-start | bytes 27656 | tf_op jit(solution)/shard_map/ppermute | solution.py:23
  11.2 6.3 %collective-permute-start.2 = (f32[4,26,1,24]{1,3,2,0:T(8,128)S(1)}, f32[4,26,1,24]{1,3,2,0:T(8,128)S(1)}, u32[]{:S(2)}, u32[]{:S(2)}) collective-permute-start(f32[4,26,1,24]{1,3,2,0:T(8,128)S(1)} %get-tuple-element.8), channel_id=1, source_target_pairs={{2,0},{4,2},{6,4},{3,1},{5,3},{7,5},{10,8},{12,10},{14,12},{11,9},... | collective-permute-start | bytes 29960 | tf_op jit(solution)/shard_map/ppermute | solution.py:25
  13.4 5.3 %collective-permute-start.3 = (f32[4,26,1,24]{1,3,2,0:T(8,128)S(1)}, f32[4,26,1,24]{1,3,2,0:T(8,128)S(1)}, u32[]{:S(2)}, u32[]{:S(2)}) collective-permute-start(f32[4,26,1,24]{1,3,2,0:T(8,128)S(1)} %get-tuple-element.7), channel_id=1, source_target_pairs={{0,2},{2,4},{4,6},{1,3},{3,5},{5,7},{8,10},{10,12},{12,14},{9,11},... | collective-permute-start | bytes 29960 | tf_op jit(solution)/shard_map/ppermute | solution.py:23
  19.3 8.7 %collective-permute-start.4 = (f32[4,26,26,1]{2,1,3,0:T(8,128)S(1)}, f32[4,26,26,1]{2,1,3,0:T(8,128)S(1)}, u32[]{:S(2)}, u32[]{:S(2)}) collective-permute-start(f32[4,26,26,1]{2,1,3,0:T(8,128)S(1)} %copy.145), channel_id=1, source_target_pairs={{1,0},{3,2},{5,4},{7,6},{9,8},{11,10},{13,12},{15,14},{17,16},{19,... | collective-permute-start | bytes 32456 | tf_op jit(solution)/shard_map/ppermute | solution.py:25
  23.9 4.3 %collective-permute-start.5 = (f32[4,26,26,1]{2,1,3,0:T(8,128)S(1)}, f32[4,26,26,1]{2,1,3,0:T(8,128)S(1)}, u32[]{:S(2)}, u32[]{:S(2)}) collective-permute-start(f32[4,26,26,1]{2,1,3,0:T(8,128)S(1)} %copy.147), channel_id=1, source_target_pairs={{0,1},{2,3},{4,5},{6,7},{8,9},{10,11},{12,13},{14,15},{16,17},{18,... | collective-permute-start | bytes 32456 | tf_op jit(solution)/shard_map/ppermute | solution.py:23
  38.6 4.8 %collective-permute-start.6 = (f32[4,1,24,24]{3,2,1,0:T(8,128)S(1)}, f32[4,1,24,24]{3,2,1,0:T(8,128)S(1)}, u32[]{:S(2)}, u32[]{:S(2)}) collective-permute-start(f32[4,1,24,24]{3,2,1,0:T(8,128)S(1)} %copy.150), channel_id=1, source_target_pairs={{0,8},{8,16},{16,24},{1,9},{9,17},{17,25},{2,10},{10,18},{18,26},{... | collective-permute-start | bytes 27656 | tf_op jit(solution)/shard_map/ppermute | solution.py:12
  44.2 6.0 %collective-permute-start.7 = (f32[4,25,1,24]{1,3,2,0:T(8,128)S(1)}, f32[4,25,1,24]{1,3,2,0:T(8,128)S(1)}, u32[]{:S(2)}, u32[]{:S(2)}) collective-permute-start(f32[4,25,1,24]{1,3,2,0:T(8,128)S(1)} %pad_maximum_fusion.35), channel_id=1, source_target_pairs={{0,2},{2,4},{4,6},{1,3},{3,5},{5,7},{8,10},{10,12},{12,14},{9,11},... | collective-permute-start | bytes 28808 | tf_op jit(solution)/shard_map/ppermute | solution.py:12
  50.5 5.1 %collective-permute-start.8 = (f32[4,25,25,1]{2,1,3,0:T(8,128)S(1)}, f32[4,25,25,1]{2,1,3,0:T(8,128)S(1)}, u32[]{:S(2)}, u32[]{:S(2)}) collective-permute-start(f32[4,25,25,1]{2,1,3,0:T(8,128)S(1)} %copy.152), channel_id=1, source_target_pairs={{0,1},{2,3},{4,5},{6,7},{8,9},{10,11},{12,13},{14,15},{16,17},{18,... | collective-permute-start | bytes 30008 | tf_op jit(solution)/shard_map/ppermute | solution.py:12
  87.2 12.4 %collective-permute-start.9 = (f32[4,1,12,12]{1,3,2,0:T(8,128)S(1)}, f32[4,1,12,12]{1,3,2,0:T(8,128)S(1)}, u32[]{:S(2)}, u32[]{:S(2)}) collective-permute-start(f32[4,1,12,12]{1,3,2,0:T(8,128)S(1)} %slice.265), channel_id=1, source_target_pairs={{0,8},{8,16},{16,24},{1,9},{9,17},{17,25},{2,10},{10,18},{18,26},{... | collective-permute-start | bytes 6920 | tf_op jit(solution)/shard_map/ppermute | solution.py:12
  99.7 5.9 %collective-permute-start.10 = (f32[4,13,1,12]{1,3,2,0:T(8,128)S(1)}, f32[4,13,1,12]{1,3,2,0:T(8,128)S(1)}, u32[]{:S(2)}, u32[]{:S(2)}) collective-permute-start(f32[4,13,1,12]{1,3,2,0:T(8,128)S(1)} %pad_maximum_fusion.39), channel_id=1, source_target_pairs={{0,2},{2,4},{4,6},{1,3},{3,5},{5,7},{8,10},{10,12},{12,14},{9,11},... | collective-permute-start | bytes 7496 | tf_op jit(solution)/shard_map/ppermute | solution.py:12
  105.7 3.8 %collective-permute-start.11 = (f32[4,13,13,1]{1,3,2,0:T(1,128)S(1)}, f32[4,13,13,1]{1,3,2,0:T(1,128)S(1)}, u32[]{:S(2)}, u32[]{:S(2)}) collective-permute-start(f32[4,13,13,1]{1,3,2,0:T(1,128)S(1)} %pad_maximum_fusion.42), channel_id=1, source_target_pairs={{0,1},{2,3},{4,5},{6,7},{8,9},{10,11},{12,13},{14,15},{16,17},{18,... | collective-permute-start | bytes 8120 | tf_op jit(solution)/shard_map/ppermute | solution.py:12
  115.0 3.4 %collective-permute-start.12 = (f32[4,25]{1,0:T(4,128)S(1)}, f32[4,25]{1,0:T(4,128)S(1)}, u32[]{:S(2)}, u32[]{:S(2)}) collective-permute-start(f32[4,25]{1,0:T(4,128)S(1)} %slice.237), channel_id=1, source_target_pairs={{1,0},{3,2},{5,4},{7,6},{9,8},{11,10},{13,12},{15,14},{17,16},{19,... | collective-permute-start | bytes 1208 | tf_op jit(solution)/shard_map/ppermute | solution.py:12
  120.8 5.8 %collective-permute-start.13 = (f32[4,30]{1,0:T(4,128)S(1)}, f32[4,30]{1,0:T(4,128)S(1)}, u32[]{:S(2)}, u32[]{:S(2)}) collective-permute-start(f32[4,30]{1,0:T(4,128)S(1)} %slice.240), channel_id=1, source_target_pairs={{2,0},{4,2},{6,4},{3,1},{5,3},{7,5},{10,8},{12,10},{14,12},{11,9},... | collective-permute-start | bytes 1448 | tf_op jit(solution)/shard_map/ppermute | solution.py:12
  138.5 4.3 %collective-permute-start.14 = (f32[4,36]{1,0:T(4,128)S(1)}, f32[4,36]{1,0:T(4,128)S(1)}, u32[]{:S(2)}, u32[]{:S(2)}) collective-permute-start(f32[4,36]{1,0:T(4,128)S(1)} %slice.243), channel_id=1, source_target_pairs={{8,0},{16,8},{24,16},{9,1},{17,9},{25,17},{10,2},{18,10},{26,18},{... | collective-permute-start | bytes 1736 | tf_op jit(solution)/shard_map/ppermute | solution.py:12
  198.0 4.4 %collective-permute-start.15 = (f32[4,36]{1,0:T(4,128)S(1)}, f32[4,36]{1,0:T(4,128)S(1)}, u32[]{:S(2)}, u32[]{:S(2)}) collective-permute-start(f32[4,36]{1,0:T(4,128)S(1)} %fusion.86), channel_id=1, source_target_pairs={{0,8},{8,16},{16,24},{1,9},{9,17},{17,25},{2,10},{10,18},{18,26},{... | collective-permute-start | bytes 1736 | tf_op jit(solution)/shard_map/ppermute | solution.py:12
  213.1 4.3 %collective-permute-start.16 = (f32[4,30]{1,0:T(4,128)S(1)}, f32[4,30]{1,0:T(4,128)S(1)}, u32[]{:S(2)}, u32[]{:S(2)}) collective-permute-start(f32[4,30]{1,0:T(4,128)S(1)} %fusion.34), channel_id=1, source_target_pairs={{0,2},{2,4},{4,6},{1,3},{3,5},{5,7},{8,10},{10,12},{12,14},{9,11},... | collective-permute-start | bytes 1448 | tf_op jit(solution)/shard_map/ppermute | solution.py:12
  220.8 3.1 %collective-permute-start.17 = (f32[4,25]{1,0:T(4,128)S(1)}, f32[4,25]{1,0:T(4,128)S(1)}, u32[]{:S(2)}, u32[]{:S(2)}) collective-permute-start(f32[4,25]{1,0:T(4,128)S(1)} %fusion.50), channel_id=1, source_target_pairs={{0,1},{2,3},{4,5},{6,7},{8,9},{10,11},{12,13},{14,15},{16,17},{18,... | collective-permute-start | bytes 1208 | tf_op jit(solution)/shard_map/ppermute | solution.py:12
  226.1 4.5 %collective-permute-start.18 = (f32[4,1,6,6]{3,2,1,0:T(8,128)S(1)}, f32[4,1,6,6]{3,2,1,0:T(8,128)S(1)}, u32[]{:S(2)}, u32[]{:S(2)}) collective-permute-start(f32[4,1,6,6]{3,2,1,0:T(8,128)S(1)} %slice.270), channel_id=1, source_target_pairs={{8,0},{16,8},{24,16},{9,1},{17,9},{25,17},{10,2},{18,10},{26,18},{... | collective-permute-start | bytes 1736 | tf_op jit(solution)/shard_map/ppermute | solution.py:12
  230.6 5.4 %collective-permute-start.19 = (f32[4,7,1,6]{3,2,1,0:T(1,128)S(1)}, f32[4,7,1,6]{3,2,1,0:T(1,128)S(1)}, u32[]{:S(2)}, u32[]{:S(2)}) collective-permute-start(f32[4,7,1,6]{3,2,1,0:T(1,128)S(1)} %slice.271), channel_id=1, source_target_pairs={{2,0},{4,2},{6,4},{3,1},{5,3},{7,5},{10,8},{12,10},{14,12},{11,9},... | collective-permute-start | bytes 2024 | tf_op jit(solution)/shard_map/ppermute | solution.py:12
  236.0 5.3 %collective-permute-start.20 = (f32[4,7,7,1]{3,2,1,0:T(8,128)S(1)}, f32[4,7,7,1]{3,2,1,0:T(8,128)S(1)}, u32[]{:S(2)}, u32[]{:S(2)}) collective-permute-start(f32[4,7,7,1]{3,2,1,0:T(8,128)S(1)} %pad_maximum_fusion.26), channel_id=1, source_target_pairs={{1,0},{3,2},{5,4},{7,6},{9,8},{11,10},{13,12},{15,14},{17,16},{19,... | collective-permute-start | bytes 2360 | tf_op jit(solution)/shard_map/ppermute | solution.py:12
  242.7 4.6 %collective-permute-start.21 = (f32[4,1,12,12]{2,0,3,1:T(4,128)S(1)}, f32[4,1,12,12]{2,0,3,1:T(4,128)S(1)}, u32[]{:S(2)}, u32[]{:S(2)}) collective-permute-start(f32[4,1,12,12]{2,0,3,1:T(4,128)S(1)} %slice.278), channel_id=1, source_target_pairs={{8,0},{16,8},{24,16},{9,1},{17,9},{25,17},{10,2},{18,10},{26,18},{... | collective-permute-start | bytes 6920 | tf_op jit(solution)/shard_map/ppermute | solution.py:12
  247.3 10.4 %collective-permute-start.22 = (f32[4,13,1,12]{2,0,3,1:T(4,128)S(1)}, f32[4,13,1,12]{2,0,3,1:T(4,128)S(1)}, u32[]{:S(2)}, u32[]{:S(2)}) collective-permute-start(f32[4,13,1,12]{2,0,3,1:T(4,128)S(1)} %pad_maximum_fusion.22), channel_id=1, source_target_pairs={{2,0},{4,2},{6,4},{3,1},{5,3},{7,5},{10,8},{12,10},{14,12},{11,9},... | collective-permute-start | bytes 7496 | tf_op jit(solution)/shard_map/ppermute | solution.py:12
  257.8 5.1 %collective-permute-start.23 = (f32[4,13,13,1]{2,0,3,1:T(4,128)S(1)}, f32[4,13,13,1]{2,0,3,1:T(4,128)S(1)}, u32[]{:S(2)}, u32[]{:S(2)}) collective-permute-start(f32[4,13,13,1]{2,0,3,1:T(4,128)S(1)} %pad_maximum_fusion.40), channel_id=1, source_target_pairs={{1,0},{3,2},{5,4},{7,6},{9,8},{11,10},{13,12},{15,14},{17,16},{19,... | collective-permute-start | bytes 8120 | tf_op jit(solution)/shard_map/ppermute | solution.py:12
  (16 other events, 285.5 us)
